TPU v7x, 32 devices: a whole 2x2x4 slice. The times are simulated.
32 devices in a mesh: gene: 8 (over z, x), cell: 4 (over y, core).
Axes of the slice: x: 2, y: 2, z: 4, core: 2. Of those that a mesh axis runs over, the one named last changes fastest.
Arguments:
- counts: bfloat16 [32768, 8192], P('gene', 'cell'), may hold values from -6 to 6
- loadings: float32 [32768, 128], P('gene'), may hold values from -0.03125 to 0.03125
- values: float32 [128], replicated, may hold values from 0.5 to 2
- test_matrix: bfloat16 [8192, 128], P('cell'), may hold values from -0.0625 to 0.0625
- tile_mask: int32 [128, 64], P('gene', 'cell'), may hold values 0 or 1
Outputs:
- new_loadings: float32 [32768, 128], P('gene')
- new_values: float32 [128], replicated
All inputs are finite; a program needn't handle non-finite values. No bound on the sum of `tile_mask` on one device may be relied on, other than what follows from the above.
Results may differ from a plain program's by a relative error of at most 0.0028.
Values sent between devices are 32-bit elements; how exact they have to be, the bound alone decides.
A program may use at most 128 MiB of HBM per device.

v0:
```python
import jax
import jax.numpy as jnp
from jax import lax
from jax.sharding import PartitionSpec as P

GENE_TILE = 256
CELL_TILE = 128
SWEEPS = 3


def contract(left, right):
    return lax.dot_general(
        left,
        right,
        (((0,), (0,)), ((), ())),
        precision=lax.Precision.HIGHEST,
        preferred_element_type=jnp.float32,
    )


def outer_rows(stacked):
    return lax.dot_general(
        stacked,
        stacked,
        (((1,), (1,)), ((), ())),
        precision=lax.Precision.HIGHEST,
        preferred_element_type=jnp.float32,
    )


def local(counts, loadings, values, test_matrix, tile_mask):
    highest = lax.Precision.HIGHEST
    gene_rows, cell_cols = counts.shape
    components = loadings.shape[1]
    sketch_width = test_matrix.shape[1]
    cells_total = cell_cols * lax.axis_size("cell")
    genes_total = gene_rows * lax.axis_size("gene")
    tile_wide = jnp.repeat(
        jnp.repeat(tile_mask.astype(jnp.bfloat16), GENE_TILE, axis=0), CELL_TILE, axis=1
    )
    masked = counts * tile_wide
    load_narrow = loadings.astype(jnp.bfloat16)
    proj_part = lax.dot_general(
        load_narrow, masked, (((0,), (0,)), ((), ())), preferred_element_type=jnp.float32
    )
    projection = lax.psum(proj_part, "gene")
    test_wide = test_matrix.astype(jnp.float32)
    raw_part = jnp.dot(masked, test_matrix, preferred_element_type=jnp.float32)
    small_part = jnp.dot(projection, test_wide, precision=highest)
    raw_sketch, small_sketch = lax.psum((raw_part, small_part), "cell")
    sketch = raw_sketch - jnp.dot(loadings, small_sketch, precision=highest)
    sketch_gram = lax.psum(contract(sketch, sketch), "gene")
    factor = jnp.linalg.cholesky(sketch_gram)
    basis_rows = jax.scipy.linalg.solve_triangular(factor, sketch.T, lower=True)
    along_loadings = jnp.dot(basis_rows, loadings, precision=highest)
    coef = lax.psum(
        jnp.dot(basis_rows, masked, precision=highest, preferred_element_type=jnp.float32)
        - jnp.dot(along_loadings, projection, precision=highest),
        "gene",
    )
    stacked = jnp.concatenate([projection, coef], axis=0)
    core_sum = lax.psum(outer_rows(stacked), "cell")
    squares = jnp.concatenate([values * values, jnp.zeros((sketch_width,), jnp.float32)])
    core_matrix = core_sum / cells_total + jnp.diag(squares)
    subspace = jnp.eye(components + sketch_width, components, dtype=jnp.float32)
    for sweep in range(SWEEPS):
        image_block = jnp.dot(core_matrix, subspace, precision=highest)
        chol = jnp.linalg.cholesky(contract(image_block, image_block))
        subspace = jax.scipy.linalg.solve_triangular(chol, image_block.T, lower=True).T
    final_image = jnp.dot(core_matrix, subspace, precision=highest)
    new_values = jnp.sqrt(jnp.sum(subspace * final_image, axis=0))
    rotated = jnp.dot(loadings, subspace[:components], precision=highest) + contract(
        basis_rows, subspace[components:]
    )
    new_loadings = rotated * genes_total**0.5
    return (new_loadings, new_values)


def solution(mesh):
    placed = (P("gene", "cell"), P("gene", None), P(), P("cell", None), P("gene", "cell"))
    return jax.shard_map(
        local, mesh=mesh, in_specs=placed, out_specs=(P("gene", None), P()), check_vma=False
    )
```

profile of v0, /device:TPU:0, one launch (start us, length us, event | category | flops | bytes accessed | tf_op | source)
XLA Modules:
  0.0 522.0 jit_solution(2787085083832913234)
XLA Ops:
  7.2 0.7 convert_element_type.8
  8.1 19.0 %broadcast_in_dim.27 = bf16[4096,16,128]{2,1,0:T(8,128)(2,1)} broadcast(bf16[4096,16]{1,0:T(8,128)(2,1)S(1)} %bitcast.89), dimensions={0,1} | broadcast | bytes 16908288 | tf_op jit(solution)/shard_map/broadcast_in_dim | solution.py:38
  27.1 14.2 %convolution_bitcast_fusion.2 = f32[128,2048]{0,1:T(8,128)} fusion(f32[4096,128]{1,0:T(8,128)S(1)} %copy-done.1, bf16[4096,2048]{1,0:T(8,128)(2,1)} %param.8, bf16[512,8,16,128]{3,2,1,0:T(8,128)(2,1)} %bitcast.86), kind=kOutput, calls=%fused_computation.7 | convolution fusion | flops 2156396544 | bytes 36700160 | tf_op jit(solution)/shard_map/dot_general | solution.py:43
  41.3 15.6 %fusion.40 = f32[4096,128]{1,0:T(8,128)} fusion(bf16[2048,128]{1,0:T(8,128)(2,1)S(1)} %copy-done, bf16[4096,2048]{1,0:T(8,128)(2,1)} %param.8, bf16[512,8,16,128]{3,2,1,0:T(8,128)(2,1)} %bitcast.87), kind=kOutput, calls=%fused_computation.65 | convolution fusion | flops 2155872256 | bytes 36175872 | tf_op jit(solution)/shard_map/dot_general | solution.py:48
  56.9 65.6 %all-reduce.8.cloned.1.call-done = f32[128,2048]{0,1:T(8,128)} async-done(((f32[128,2048]{0,1:T(8,128)}), f32[128,2048]{0,1:T(8,128)}) %all-reduce.8.cloned.1.call-update) | async-done | bytes 1048592 | tf_op jit(solution)/shard_map/psum | solution.py:46
  122.5 2.8 fusion.41
  125.4 0.6 all-reduce.10.cloned.1.call-start
  126.0 51.7 %all-reduce.16.cloned.1.call-done = (f32[4096,128]{1,0:T(8,128)}, f32[128,128]{1,0:T(8,128)}) async-done(((f32[4096,128]{1,0:T(8,128)}, f32[128,128]{1,0:T(8,128)}), (f32[4096,128]{1,0:T(8,128)}, f32[128,128]{1,0:T(8,128)})) %all-reduce.16.cloned.1.call-update) | async-done | bytes 2162704 | tf_op jit(solution)/shard_map/psum | solution.py:50
  177.7 4.0 fusion.1
  181.7 4.1 fusion.42
  186.0 69.3 %all-reduce.10.cloned.1.call-done = f32[128,128]{0,1:T(8,128)} async-done(((f32[128,128]{0,1:T(8,128)}), f32[128,128]{0,1:T(8,128)}) %all-reduce.10.cloned.1.call-update) | async-done | bytes 65552 | tf_op jit(solution)/shard_map/psum | solution.py:52
  255.3 0.9 copy.9
  256.3 0.9 fusion.29
  257.1 11.7 %cholesky.74 = f32[128,128]{1,0:T(8,128)S(1)} custom-call(f32[128,128]{1,0:T(8,128)S(1)} %fusion.29), custom_call_target="Cholesky" | custom-call | tf_op jit(solution)/shard_map/jit(cholesky)/cholesky | solution.py:53
  268.9 0.6 compare_reduce_fusion.3
  269.5 0.7 fusion.15
  270.2 9.8 %custom-call.9 = f32[1,128,128]{1,2,0:T(8,128)S(1)} custom-call(f32[1,128,128]{2,1,0:T(8,128)S(1)} %fusion.15), custom_call_target="InvertDiagBlocksLowerTriangular" | custom-call | tf_op jit(solution)/shard_map/jit(_solve_triangular)/triangular_solve | solution.py:54
  280.0 3.3 fusion.27
  283.2 27.7 %fusion.39 = f32[128,2048]{0,1:T(8,128)} fusion(f32[128,4096]{1,0:T(8,128)} %fusion.27, bf16[4096,2048]{1,0:T(8,128)(2,1)} %param.8, bf16[512,8,16,128]{3,2,1,0:T(8,128)(2,1)} %bitcast.88), kind=kOutput, calls=%fused_computation.64 | convolution fusion | flops 12893290496 | bytes 36700160 | tf_op jit(solution)/shard_map/dot_general | solution.py:57
  310.9 3.9 fusion.43
  314.9 2.0 convolution_subtract_fusion
  316.9 0.5 all-reduce.14.cloned.1.call-start
  317.4 77.8 %all-reduce.12.cloned.1.call-done = f32[128,2048]{0,1:T(8,128)} async-done(((f32[128,2048]{0,1:T(8,128)}), f32[128,2048]{0,1:T(8,128)}) %all-reduce.12.cloned.1.call-update) | async-done | bytes 1048592 | tf_op jit(solution)/shard_map/psum | solution.py:56
  395.2 6.4 %fusion.2 = f32[256,256]{1,0:T(8,128)} fusion(f32[128,2048]{0,1:T(8,128)} %all-reduce.12.cloned.1.call-done, f32[128,2048]{0,1:T(8,128)} %all-reduce.8.cloned.1.call-done), kind=kOutput, calls=%fused_computation.8 | convolution fusion | flops 1611137024 | bytes 2359296 | tf_op jit(solution)/shard_map/dot_general | solution.py:22
  401.6 32.0 %all-reduce.14.cloned.1.call-done = f32[256,256]{1,0:T(8,128)} async-done(((f32[256,256]{1,0:T(8,128)}), f32[256,256]{1,0:T(8,128)}) %all-reduce.14.cloned.1.call-update) | async-done | bytes 262160 | tf_op jit(solution)/shard_map/psum | solution.py:62
  433.6 1.3 fusion.14
  435.0 0.4 fusion.44
  435.5 11.7 %cholesky.85 = f32[128,128]{1,0:T(8,128)S(1)} custom-call(f32[128,128]{1,0:T(8,128)S(1)} %fusion.26), custom_call_target="Cholesky" | custom-call | tf_op jit(solution)/shard_map/jit(cholesky)/cholesky | solution.py:68
  447.2 0.6 compare_reduce_fusion.2
  447.9 0.7 fusion.16
  448.5 9.8 %custom-call.12 = f32[1,128,128]{1,2,0:T(8,128)S(1)} custom-call(f32[1,128,128]{2,1,0:T(8,128)S(1)} %fusion.16), custom_call_target="InvertDiagBlocksLowerTriangular" | custom-call | tf_op jit(solution)/shard_map/jit(_solve_triangular)/triangular_solve | solution.py:69
  458.7 1.4 fusion.38
  460.0 0.4 fusion.45
  460.5 11.9 %cholesky.96 = f32[128,128]{1,0:T(8,128)S(1)} custom-call(f32[128,128]{1,0:T(8,128)S(1)} %fusion.24), custom_call_target="Cholesky" | custom-call | tf_op jit(solution)/shard_map/jit(cholesky)/cholesky | solution.py:68
  472.5 0.6 compare_reduce_fusion.1
  473.1 0.7 fusion.17
  473.8 9.8 %custom-call.13 = f32[1,128,128]{1,2,0:T(8,128)S(1)} custom-call(f32[1,128,128]{2,1,0:T(8,128)S(1)} %fusion.17), custom_call_target="InvertDiagBlocksLowerTriangular" | custom-call | tf_op jit(solution)/shard_map/jit(_solve_triangular)/triangular_solve | solution.py:69
  483.9 0.4 fusion.37
  484.3 0.4 fusion.46
  484.8 11.7 %cholesky.107 = f32[128,128]{1,0:T(8,128)S(1)} custom-call(f32[128,128]{1,0:T(8,128)S(1)} %fusion.22), custom_call_target="Cholesky" | custom-call | tf_op jit(solution)/shard_map/jit(cholesky)/cholesky | solution.py:68
  496.6 0.6 compare_reduce_fusion
  497.2 0.7 fusion.18
  497.9 10.0 %custom-call.14 = f32[1,128,128]{1,2,0:T(8,128)S(1)} custom-call(f32[1,128,128]{2,1,0:T(8,128)S(1)} %fusion.18), custom_call_target="InvertDiagBlocksLowerTriangular" | custom-call | tf_op jit(solution)/shard_map/jit(_solve_triangular)/triangular_solve | solution.py:69
  508.2 0.6 fusion.6
  508.8 0.5 sqrt.3
  509.3 2.0 convolution_bitcast_fusion
  511.3 2.1 fusion
  513.4 1.8 copy.15
  (40 shorter events, 1.9 us)
Async XLA Ops:
  7.2 34.2 %copy-start = (bf16[2048,128]{1,0:T(8,128)(2,1)S(1)}, bf16[2048,128]{1,0:T(8,128)(2,1)}, u32[]{:S(2)}) copy-start(bf16[2048,128]{1,0:T(8,128)(2,1)} %param.11) | copy-start | bytes 1572868
  7.2 115.3 %all-reduce.8.cloned.1.call-start = ((), (), s32[]{:S(2)}) async-start(), calls=%async_computation | async-start | bytes 2097152 | tf_op jit(solution)/shard_map/psum | solution.py:46
  8.1 19.0 %copy-start.1 = (f32[4096,128]{1,0:T(8,128)S(1)}, f32[4096,128]{1,0:T(8,128)}, u32[]{:S(2)}) copy-start(f32[4096,128]{1,0:T(8,128)} %param.9) | copy-start | bytes 6291460
  41.3 136.4 %all-reduce.16.cloned.1.call-start = ((), (), s32[]{:S(2)}) async-start(), calls=%async_computation.4 | async-start | bytes 4325376 | tf_op jit(solution)/shard_map/psum | solution.py:50
  125.4 129.9 %all-reduce.10.cloned.1.call-start = ((), (), s32[]{:S(2)}) async-start(), calls=%async_computation.1 | async-start | bytes 131072 | tf_op jit(solution)/shard_map/psum | solution.py:52
  185.8 209.4 %all-reduce.12.cloned.1.call-start = ((), (), s32[]{:S(2)}) async-start(), calls=%async_computation.2 | async-start | bytes 2097152 | tf_op jit(solution)/shard_map/psum | solution.py:56
  283.2 27.7 %copy-start.2 = (f32[4096,128]{1,0:T(8,128)S(1)}, f32[4096,128]{1,0:T(8,128)}, u32[]{:S(2)}) copy-start(f32[4096,128]{1,0:T(8,128)} %param.9) | copy-start | bytes 6291460
  310.9 3.9 copy-start.4
  310.9 3.9 copy-start.6
  316.9 84.7 %copy-start.7 = (f32[128]{0:T(128)S(1)}, f32[128]{0:T(128)}, u32[]{:S(2)}) copy-start(f32[128]{0:T(128)} %param.10) | copy-start | bytes 1540
  316.9 116.7 %all-reduce.14.cloned.1.call-start = ((), (), s32[]{:S(2)}) async-start(), calls=%async_computation.3 | async-start | bytes 524288 | tf_op jit(solution)/shard_map/psum | solution.py:62
  433.6 50.3 %copy-start.5 = (f32[256,256]{1,0:T(8,128)S(1)}, f32[256,256]{1,0:T(8,128)}, u32[]{:S(2)}) copy-start(f32[256,256]{1,0:T(8,128)} %all-reduce.14.cloned.1.call-done) | copy-start | bytes 786436
  509.3 2.0 copy-start.3
Sparse Core Ops, SparseCore 0:
  41.4 81.0 all-reduce.7
  125.6 52.0 all-reduce.15
  185.9 69.3 all-reduce.9
  317.0 78.1 all-reduce.11
  401.7 31.8 all-reduce.13
where the time goes:
time: 529 us; the launch traced here: 522 us
  waiting for transfers between devices  296 us (56%)
  matrix products  93.8 us (18%)
  other arithmetic  93.4 us (18%)
  local copies, waits for them, and re-layouts  22.7 us (4%)
  between operations  14.3 us (3%)
    psum x1, waiting for transfers between devices, local(): lax.psum(jnp.dot(basis_rows, masked, precision=highest, preferred_element...  77.8 us
    psum x1, waiting for transfers between devices, local(): sketch_gram = lax.psum(contract(sketch, sketch), 'gene')  69.3 us
    psum x1, waiting for transfers between devices, local(): projection = lax.psum(proj_part, 'gene')  65.6 us
    psum x1, waiting for transfers between devices, local(): raw_sketch, small_sketch = lax.psum((raw_part, small_part), 'cell')  51.7 us
    another operation x9, other arithmetic, local(): chol = jnp.linalg.cholesky(contract(image_block, image_block))  37.3 us
    psum x1, waiting for transfers between devices, local(): core_sum = lax.psum(outer_rows(stacked), 'cell')  32 us
    another operation x6, other arithmetic, local(): jax.scipy.linalg.solve_triangular(chol, image_block.T, lower=True)  31.6 us
    dot_general x1, matrix products, local(): jnp.dot(basis_rows, masked, precision=highest, preferred_element_type=jnp...  27.7 us
  transfers between devices with their start and end apart: 5, of which 5 were waited for; matrix products, arithmetic and copies ran while one was open for 3% of the time, Pallas kernels for 0%

commit v1 on v0

v1 whole, which is shorter than its diff:
```python
import functools

import jax
import jax.numpy as jnp
from jax import lax
from jax.experimental import pallas as pl
from jax.experimental.pallas import tpu as pltpu
from jax.sharding import PartitionSpec as P

GENE_TILE = 256
CELL_TILE = 128
SWEEPS = 3
ROW_BLOCK = 512
CHUNKS = 8
HIGH = lax.Precision.HIGHEST
MESH = pl.DeviceIdType.MESH
LIMIT = 60 * 1024 * 1024
VMEM = pl.BlockSpec(memory_space=pltpu.VMEM)


def dot(a, b, dims=((1,), (0,)), precision=HIGH):
    return lax.dot_general(
        a, b, (dims, ((), ())), precision=precision, preferred_element_type=jnp.float32
    )


def split(a):
    high = a.astype(jnp.bfloat16)
    return high, (a - high.astype(jnp.float32)).astype(jnp.bfloat16)


def masked_rows(counts_ref, mask_ref, step):
    parts = []
    per_block = ROW_BLOCK // GENE_TILE
    for part in range(per_block):
        row = mask_ref[step * per_block + part].astype(jnp.bfloat16)
        parts.append(counts_ref[pl.ds(part * GENE_TILE, GENE_TILE), :] * row)
    return jnp.concatenate(parts, axis=0)


def first_kernel(counts_ref, mask_ref, load_ref, test_ref, y_ref, p_ref, z_ref):
    step = pl.program_id(0)
    masked = masked_rows(counts_ref, mask_ref, step)
    y_ref[...] = dot(masked, test_ref[...], precision=None)
    part = dot(load_ref[...].astype(jnp.bfloat16), masked, ((0,), (0,)), None)

    @pl.when(step == 0)
    def _():
        p_ref[...] = part

    @pl.when(step > 0)
    def _():
        p_ref[...] += part

    @pl.when(step == pl.num_programs(0) - 1)
    def _():
        high, low = split(p_ref[...])
        z_ref[...] = dot(high, test_ref[...], precision=None) + dot(
            low, test_ref[...], precision=None
        )


def first_pass(counts, mask_rows, loadings, test_matrix):
    rows, cols = counts.shape
    comps, width = loadings.shape[1], test_matrix.shape[1]
    return pl.pallas_call(
        first_kernel,
        grid=(rows // ROW_BLOCK,),
        in_specs=[
            pl.BlockSpec((ROW_BLOCK, cols), lambda i: (i, 0)),
            pl.BlockSpec(mask_rows.shape, lambda i: (0, 0, 0)),
            pl.BlockSpec((ROW_BLOCK, comps), lambda i: (i, 0)),
            pl.BlockSpec(test_matrix.shape, lambda i: (0, 0)),
        ],
        out_specs=[
            pl.BlockSpec((ROW_BLOCK, width), lambda i: (i, 0)),
            pl.BlockSpec((comps, cols), lambda i: (0, 0)),
            pl.BlockSpec((comps, width), lambda i: (0, 0)),
        ],
        out_shape=[
            jax.ShapeDtypeStruct((rows, width), jnp.float32),
            jax.ShapeDtypeStruct((comps, cols), jnp.float32),
            jax.ShapeDtypeStruct((comps, width), jnp.float32),
        ],
        compiler_params=pltpu.CompilerParams(vmem_limit_bytes=LIMIT),
        name="first_pass",
    )(counts, mask_rows, loadings, test_matrix)


def second_kernel(share, counts_ref, mask_ref, load_ref, y_ref, z_ref, s_ref, d_ref, ga_ref):
    step = pl.program_id(0)
    masked = masked_rows(counts_ref, mask_ref, step)
    load = load_ref[...]
    sketch = y_ref[...] - dot(load, z_ref[...])
    s_ref[...] = sketch
    high, low = split(sketch)
    both = dot(jnp.concatenate([high, low], axis=1), masked, ((0,), (0,)), None)
    width = sketch.shape[1]
    part = both[:width] + both[width:]
    small = (
        dot(jnp.concatenate([sketch, load], axis=1), sketch, ((0,), (0,))) * share
    )

    @pl.when(step == 0)
    def _():
        d_ref[...] = part
        ga_ref[...] = small

    @pl.when(step > 0)
    def _():
        d_ref[...] += part
        ga_ref[...] += small


def second_pass(counts, mask_rows, loadings, y, z, share):
    rows, cols = counts.shape
    comps, width = loadings.shape[1], y.shape[1]
    return pl.pallas_call(
        functools.partial(second_kernel, share),
        grid=(rows // ROW_BLOCK,),
        in_specs=[
            pl.BlockSpec((ROW_BLOCK, cols), lambda i: (i, 0)),
            pl.BlockSpec(mask_rows.shape, lambda i: (0, 0, 0)),
            pl.BlockSpec((ROW_BLOCK, comps), lambda i: (i, 0)),
            pl.BlockSpec((ROW_BLOCK, width), lambda i: (i, 0)),
            pl.BlockSpec(z.shape, lambda i: (0, 0)),
        ],
        out_specs=[
            pl.BlockSpec((ROW_BLOCK, width), lambda i: (i, 0)),
            pl.BlockSpec((width, cols), lambda i: (0, 0)),
            pl.BlockSpec((width + comps, width), lambda i: (0, 0)),
        ],
        out_shape=[
            jax.ShapeDtypeStruct((rows, width), jnp.float32),
            jax.ShapeDtypeStruct((width, cols), jnp.float32),
            jax.ShapeDtypeStruct((width + comps, width), jnp.float32),
        ],
        compiler_params=pltpu.CompilerParams(vmem_limit_bytes=LIMIT),
        name="second_pass",
    )(counts, mask_rows, loadings, y, z)


class Group:
    def __init__(self, axis):
        self.axis = axis
        self.size = lax.axis_size(axis)
        self.me = lax.axis_index(axis)

    def peer(self, offset):
        return lax.rem(self.me + offset, self.size)

    def greet(self, barrier):
        for offset in range(1, self.size):
            pl.semaphore_signal(
                barrier, inc=1, device_id={self.axis: self.peer(offset)}, device_id_type=MESH
            )
        return self.size - 1

    def send(self, source, target, sems):
        copies = []
        for offset in range(1, self.size):
            peer = self.peer(offset)
            copy = pltpu.make_async_remote_copy(
                src_ref=source(peer),
                dst_ref=target,
                send_sem=sems.at[0, offset],
                recv_sem=sems.at[1, offset],
                device_id={self.axis: peer},
                device_id_type=MESH,
            )
            copy.start()
            copies.append(copy)
        return copies


def received(copies):
    for copy in copies:
        copy.wait_recv()


def sent(copies):
    for copy in copies:
        copy.wait_send()


def ordered_sum(slots, count):
    total = slots[0]
    for index in range(1, count):
        total = total + slots[index]
    return total


def rows_of(ref, index, count):
    return ref.at[pl.ds(pl.multiple_of(index * count, 8), count), :]


def cols_of(ref, index, count):
    return ref.at[:, pl.ds(pl.multiple_of(index * count, 128), count)]


def gather_kernel(
    y_in, p_in, z_in, y_out, p_out, z_out,
    z_cell, z_gene, p_slots, pair_slots, chip_slots,
    zc_sems, zg_sems, za_sems, p_sems, pair_sems, chip_sems, back_sems,
):
    gene, cell = Group("gene"), Group("cell")
    barrier = pltpu.get_barrier_semaphore()
    pl.semaphore_wait(barrier, gene.greet(barrier) + cell.greet(barrier))
    chips = cell.size // 2
    core = lax.rem(cell.me, 2)
    chip = cell.me // 2
    partner = cell.me + 1 - 2 * core
    rows = y_in.shape[0]
    half = rows // 2
    chunk = half // CHUNKS
    zrows = z_in.shape[0] // cell.size
    wide = p_in.shape[1] // gene.size

    def to(device, source, target, sems, *index):
        copy = pltpu.make_async_remote_copy(
            src_ref=source,
            dst_ref=target,
            send_sem=sems.at[(0,) + index],
            recv_sem=sems.at[(1,) + index],
            device_id={"cell": device},
            device_id_type=MESH,
        )
        copy.start()
        return copy

    pending = []
    z_first = cell.send(lambda q: rows_of(z_in, q, zrows), z_cell.at[cell.me], zc_sems)
    z_cell[cell.me] = rows_of(z_in, cell.me, zrows)[...]
    pairs = []
    for j in range(CHUNKS):
        start = pl.multiple_of((1 - core) * half + j * chunk, 8)
        pairs.append(
            to(partner, y_in.at[pl.ds(start, chunk), :],
               pair_slots.at[pl.ds(j * chunk, chunk), :], pair_sems, j)
        )
    received(z_first)
    z_gene[gene.me] = ordered_sum(z_cell, cell.size)
    z_second = gene.send(lambda q: z_gene.at[gene.me], z_gene.at[gene.me], zg_sems)
    p_copies = gene.send(lambda q: cols_of(p_in, q, wide), p_slots.at[gene.me], p_sems)
    p_slots[gene.me] = cols_of(p_in, gene.me, wide)[...]
    across = []
    for j in range(CHUNKS):
        start = pl.multiple_of(core * half + j * chunk, 8)
        pairs[j].wait_recv()
        span = pl.ds(j * chunk, chunk)
        chip_slots[chip, span, :] = y_in[pl.ds(start, chunk), :] + pair_slots[span, :]
        block = chip_slots.at[chip, span, :]
        for offset in range(1, chips):
            other = lax.rem(chip + offset, chips) * 2 + core
            across.append(to(other, block, block, chip_sems, offset, j))
    received(z_second)
    rows_of(z_out, cell.me, zrows)[...] = ordered_sum(z_gene, gene.size)
    block = rows_of(z_out, cell.me, zrows)
    z_third = cell.send(lambda q: block, block, za_sems)
    backs = []
    for j in range(CHUNKS):
        received(across[j * (chips - 1):(j + 1) * (chips - 1)])
        span = pl.ds(j * chunk, chunk)
        total = chip_slots[0, span, :]
        for index in range(1, chips):
            total = total + chip_slots[index, span, :]
        start = pl.multiple_of(core * half + j * chunk, 8)
        y_out[pl.ds(start, chunk), :] = total
        block = y_out.at[pl.ds(start, chunk), :]
        backs.append(to(partner, block, block, back_sems, j))
    received(z_third)
    received(p_copies)
    p_out[...] = ordered_sum(p_slots, gene.size)
    received(backs)
    sent(z_first + pairs + z_second + p_copies + across + z_third + backs)


def gather(y, p, z):
    genes, cells = lax.axis_size("gene"), lax.axis_size("cell")
    rows, width = y.shape
    comps, cols = p.shape
    dma = pltpu.SemaphoreType.DMA
    return pl.pallas_call(
        gather_kernel,
        in_specs=[VMEM] * 3,
        out_specs=[VMEM] * 3,
        out_shape=[
            jax.ShapeDtypeStruct(y.shape, jnp.float32),
            jax.ShapeDtypeStruct((comps, cols // genes), jnp.float32),
            jax.ShapeDtypeStruct(z.shape, jnp.float32),
        ],
        scratch_shapes=[
            pltpu.VMEM((cells, comps // cells, width), jnp.float32),
            pltpu.VMEM((genes, comps // cells, width), jnp.float32),
            pltpu.VMEM((genes, comps, cols // genes), jnp.float32),
            pltpu.VMEM((rows // 2, width), jnp.float32),
            pltpu.VMEM((cells // 2, rows // 2, width), jnp.float32),
            dma((2, cells)),
            dma((2, genes)),
            dma((2, cells)),
            dma((2, genes)),
            dma((2, CHUNKS)),
            dma((2, cells // 2, CHUNKS)),
            dma((2, CHUNKS)),
        ],
        compiler_params=pltpu.CompilerParams(
            collective_id=1, has_side_effects=True, vmem_limit_bytes=LIMIT
        ),
        name="gather",
    )(y, p, z)


def core_kernel(
    d_in, p_ref, ga_ref, out_ref,
    d_slots, parts, c_slots, g_slots,
    d_sems, c_sems, g_sems, ga_sems, ca_sems,
):
    gene, cell = Group("gene"), Group("cell")
    barrier = pltpu.get_barrier_semaphore()
    pl.semaphore_wait(barrier, gene.greet(barrier) + cell.greet(barrier))
    wide = d_in.shape[1] // gene.size
    d_copies = gene.send(lambda q: cols_of(d_in, q, wide), d_slots.at[gene.me], d_sems)
    d_slots[gene.me] = cols_of(d_in, gene.me, wide)[...]
    proj = p_ref[...]
    comps = proj.shape[0]
    width = d_in.shape[0]
    total_rows = parts.shape[0]
    small = 3 * comps + ga_ref.shape[0]
    parts[pl.ds(0, comps), :] = dot(proj, proj, ((1,), (1,)))
    parts[pl.ds(3 * comps, ga_ref.shape[0]), :] = ga_ref[...]
    if total_rows > small:
        parts[pl.ds(small, total_rows - small), :] = jnp.zeros(
            (total_rows - small, comps), jnp.float32
        )
    received(d_copies)
    inner = ordered_sum(d_slots, gene.size)
    parts[pl.ds(comps, comps), :] = dot(proj, inner, ((1,), (1,)))
    parts[pl.ds(2 * comps, width), :] = dot(inner, inner, ((1,), (1,)))
    c_rows = total_rows // cell.size
    g_rows = c_rows // gene.size
    first = cell.send(lambda q: rows_of(parts, q, c_rows), c_slots.at[cell.me], c_sems)
    c_slots[cell.me] = rows_of(parts, cell.me, c_rows)[...]
    received(first)
    sent(first)
    mine = rows_of(parts, cell.me, c_rows)
    mine[...] = ordered_sum(c_slots, cell.size)
    second = gene.send(lambda q: rows_of(mine, q, g_rows), g_slots.at[gene.me], g_sems)
    g_slots[gene.me] = rows_of(mine, gene.me, g_rows)[...]
    received(second)
    done = rows_of(rows_of(out_ref, cell.me, c_rows), gene.me, g_rows)
    done[...] = ordered_sum(g_slots, gene.size)
    third = gene.send(lambda q: done, done, ga_sems)
    received(third)
    block = rows_of(out_ref, cell.me, c_rows)
    fourth = cell.send(lambda q: block, block, ca_sems)
    received(fourth)
    sent(d_copies + second + third + fourth)


def core_sums(d, p, ga):
    genes, cells = lax.axis_size("gene"), lax.axis_size("cell")
    comps, wide = p.shape
    width = d.shape[0]
    unit = 8 * genes * cells
    total_rows = -(-(3 * comps + ga.shape[0]) // unit) * unit
    dma = pltpu.SemaphoreType.DMA
    return pl.pallas_call(
        core_kernel,
        in_specs=[VMEM] * 3,
        out_specs=VMEM,
        out_shape=jax.ShapeDtypeStruct((total_rows, comps), jnp.float32),
        scratch_shapes=[
            pltpu.VMEM((genes, width, wide), jnp.float32),
            pltpu.VMEM((total_rows, comps), jnp.float32),
            pltpu.VMEM((cells, total_rows // cells, comps), jnp.float32),
            pltpu.VMEM((genes, total_rows // cells // genes, comps), jnp.float32),
            dma((2, genes)),
            dma((2, cells)),
            dma((2, genes)),
            dma((2, genes)),
            dma((2, cells)),
        ],
        compiler_params=pltpu.CompilerParams(
            collective_id=2, has_side_effects=True, vmem_limit_bytes=LIMIT
        ),
        name="core_sums",
    )(d, p, ga)


def inverse_factor(gram):
    order = gram.shape[0]
    lane = lax.broadcasted_iota(jnp.int32, (1, order), 1)
    below = lax.broadcasted_iota(jnp.int32, (8, 1), 0)
    blocks = [gram[8 * b:8 * b + 8] for b in range(order // 8)]
    for k in range(order):
        home, spot = k // 8, k % 8
        pivot_row = blocks[home][spot:spot + 1]
        scaled = jnp.where(lane == k, 1.0, pivot_row) * (1.0 / pivot_row[:, k:k + 1])
        for b in range(home, order // 8):
            column = blocks[b][:, k:k + 1]
            kept = jnp.where(lane == k, 0.0, blocks[b])
            changed = kept - column * scaled
            if b == home:
                changed = jnp.where(below > spot, changed, blocks[b])
            blocks[b] = changed
    full = jnp.concatenate(blocks, axis=0)
    row = lax.broadcasted_iota(jnp.int32, (order, order), 0)
    col = lax.broadcasted_iota(jnp.int32, (order, order), 1)
    pivots = jnp.sum(jnp.where(row == col, full, 0.0), axis=1, keepdims=True)
    unit = jnp.where(col < row, full, jnp.where(col == row, 1.0, 0.0))
    return unit * lax.rsqrt(pivots)


def small_kernel(cells_total, sums_ref, values_ref, mix_ref, new_values_ref, core_ref, sub_ref, inv_ref):
    comps = values_ref.shape[1]
    pp = sums_ref[pl.ds(0, comps), :]
    pd = sums_ref[pl.ds(comps, comps), :]
    dd = sums_ref[pl.ds(2 * comps, comps), :]
    gram = sums_ref[pl.ds(3 * comps, comps), :]
    along_t = sums_ref[pl.ds(4 * comps, comps), :]
    inv_ref[...] = inverse_factor(gram)
    inv = inv_ref[...]
    cross = dot(pd, along_t, ((0,), (0,)))
    shifted = dot(pp, along_t)
    pc = dot(pd - shifted, inv, ((1,), (1,)))
    inner = dd - cross - cross.T + dot(along_t, shifted, ((0,), (0,)))
    cc = dot(dot(inv, inner), inv, ((1,), (1,)))
    row = lax.broadcasted_iota(jnp.int32, (comps, comps), 0)
    col = lax.broadcasted_iota(jnp.int32, (comps, comps), 1)
    values = values_ref[...]
    squares = jnp.where(row == col, values * values, 0.0)
    scale = 1.0 / cells_total
    core_ref[pl.ds(0, comps), pl.ds(0, comps)] = pp * scale + squares
    core_ref[pl.ds(0, comps), pl.ds(comps, comps)] = pc * scale
    core_ref[pl.ds(comps, comps), pl.ds(0, comps)] = pc.T * scale
    core_ref[pl.ds(comps, comps), pl.ds(comps, comps)] = cc * scale
    sub_ref[pl.ds(0, comps), :] = jnp.where(row == col, 1.0, 0.0)
    sub_ref[pl.ds(comps, comps), :] = jnp.zeros((comps, comps), jnp.float32)

    def sweep(index, carry):
        image = dot(core_ref[...], sub_ref[...])
        step = inverse_factor(dot(image, image, ((0,), (0,))))
        sub_ref[...] = dot(image, step, ((1,), (1,)))
        return carry

    lax.fori_loop(0, SWEEPS, sweep, 0)
    sub = sub_ref[...]
    image = dot(core_ref[...], sub)
    new_values_ref[...] = jnp.sqrt(jnp.sum(sub * image, axis=0, keepdims=True))
    mix_ref[pl.ds(0, comps), :] = sub[:comps]
    mix_ref[pl.ds(comps, comps), :] = dot(inv_ref[...], sub[comps:], ((0,), (0,)))


def small(sums, values, cells_total):
    comps = values.shape[0]
    return pl.pallas_call(
        functools.partial(small_kernel, cells_total),
        in_specs=[VMEM] * 2,
        out_specs=[VMEM] * 2,
        out_shape=[
            jax.ShapeDtypeStruct((2 * comps, comps), jnp.float32),
            jax.ShapeDtypeStruct((1, comps), jnp.float32),
        ],
        scratch_shapes=[
            pltpu.VMEM((2 * comps, 2 * comps), jnp.float32),
            pltpu.VMEM((2 * comps, comps), jnp.float32),
            pltpu.VMEM((comps, comps), jnp.float32),
        ],
        name="small",
    )(sums, values.reshape(1, comps))


def local(counts, loadings, values, test_matrix, tile_mask):
    gene_rows, cell_cols = counts.shape
    comps = loadings.shape[1]
    genes_total = gene_rows * lax.axis_size("gene")
    cells = lax.axis_size("cell")
    mask_rows = jnp.repeat(tile_mask.astype(jnp.float32), CELL_TILE, axis=1)[:, None, :]
    y, p, z = first_pass(counts, mask_rows, loadings, test_matrix)
    y, p, z = gather(y, p, z)
    sketch, d, ga = second_pass(counts, mask_rows, loadings, y, z, 1.0 / cells)
    sums = core_sums(d, p, ga)
    mix, new_values = small(sums, values, cell_cols * cells)
    root = genes_total**0.5
    rotated = jnp.dot(loadings, mix[:comps], precision=HIGH) + jnp.dot(
        sketch, mix[comps:], precision=HIGH
    )
    return rotated * root, new_values.reshape(comps)


def solution(mesh):
    placed = (P("gene", "cell"), P("gene", None), P(), P("cell", None), P("gene", "cell"))
    return jax.shard_map(
        local, mesh=mesh, in_specs=placed, out_specs=(P("gene", None), P()), check_vma=False
    )
```

time: 529 us -> 180 us (0.34); the launches traced: 522 us -> 179 us
  waiting for transfers between devices: 296 us -> 0 us
  Pallas kernels: 0 us -> 170 us
  other arithmetic: 93.4 us -> 0.7 us
  matrix products: 93.8 us -> 5.09 us
  local copies, waits for them, and re-layouts: 22.7 us -> 2.57 us
  between operations: 14.3 us -> 0.69 us
    psum x5 -> x0, waiting for transfers between devices: 296 us -> none  [the longest x1 77.8 us: local(): lax.psum(jnp.dot(basis_rows, masked, precision=highest, preferred_element...]
    pallas_call x0 -> x5, Pallas kernels: none -> 170 us  [the longest x1 50 us: small(): pl.pallas_call(functools.partial(small_kernel, cells_total), in_specs=[VM...]
    another operation x20 -> x0, other arithmetic: 91.8 us -> none  [the longest x9 37.3 us: local(): chol = jnp.linalg.cholesky(contract(image_block, image_block))]
    dot_general x18 -> x2, matrix products: 89.6 us -> 5.09 us  [the longest x1 2.94 us: local(): jnp.dot(loadings, mix[:comps], precision=HIGH)]
    broadcast_in_dim x2 -> x1, local copies, waits for them, and re-layouts: 19.1 us -> 0.75 us  [local(): jnp.repeat(tile_mask.astype(jnp.float32), CELL_TILE, axis=1)[:, None, :]]
  transfers between devices with their start and end apart: 5 -> 0, of which waited for: 5 -> 0; matrix products, arithmetic and copies ran while one was open for 3% -> 0% of each run, Pallas kernels for 0% -> 0%
where the time goes in v1:
time: 180 us; the launch traced here: 179 us
  Pallas kernels  170 us (94%)
  matrix products  5.09 us (3%)
  local copies, waits for them, and re-layouts  2.57 us (1%)
    pallas_call x1, Pallas kernels, small(): pl.pallas_call(functools.partial(small_kernel, cells_total), in_specs=[VM...  50 us
    pallas_call x1, Pallas kernels, core_sums(): pl.pallas_call(core_kernel, in_specs=[VMEM] * 3, out_specs=VMEM, out_shap...  48.1 us
    pallas_call x1, Pallas kernels, gather(): pl.pallas_call(gather_kernel, in_specs=[VMEM] * 3, out_specs=[VMEM] * 3,...  39 us
    pallas_call x1, Pallas kernels, second_pass(): pl.pallas_call(functools.partial(second_kernel, share), grid=(rows // ROW...  18.9 us
    pallas_call x1, Pallas kernels, first_pass(): pl.pallas_call(first_kernel, grid=(rows // ROW_BLOCK,), in_specs=[pl.Bloc...  14.2 us

profile of v1, /device:TPU:0, one launch (start us, length us, event | category | flops | bytes accessed | tf_op | source)
XLA Modules:
  0.0 179.2 jit_solution(14188686585983918074)
XLA Ops:
  0.6 0.7 convert_element_type.3
  1.3 0.7 broadcast_in_dim.3
  2.1 14.2 %first_pass.1 = (f32[4096,128]{1,0:T(8,128)}, f32[128,2048]{1,0:T(8,128)}, f32[128,128]{1,0:T(8,128)}) custom-call(bf16[4096,2048]{1,0:T(8,128)(2,1)} %counts_ref.3, f32[16,1,2048]{2,1,0:T(1,128)} %bitcast.7, f32[4096,128]{1,0:T(8,128)} %load_ref.3, bf16[2048,128]{1,0:T(8,128)(2,1)} %test_ref.1), custom_call_target="tpu_custom_call" | custom-call | tf_op jit(solution)/shard_map/first_pass/pallas_call | solution.py:66
  16.3 39.0 %gather.1 = (f32[4096,128]{1,0:T(8,128)}, f32[128,256]{1,0:T(8,128)}, f32[128,128]{1,0:T(8,128)}) custom-call(f32[4096,128]{1,0:T(8,128)} %get-tuple-element.13.y_in, f32[128,2048]{1,0:T(8,128)} %get-tuple-element.14.p_in, f32[128,128]{1,0:T(8,128)} %get-tuple-element.15.z_in), custom_call_target="tpu_custom_call" | custom-call | tf_op jit(solution)/shard_map/gather/pallas_call | solution.py:283
  55.3 18.9 %second_pass.1 = (f32[4096,128]{1,0:T(8,128)}, f32[128,2048]{1,0:T(8,128)}, f32[256,128]{1,0:T(8,128)}) custom-call(bf16[4096,2048]{1,0:T(8,128)(2,1)} %counts_ref.3, f32[16,1,2048]{2,1,0:T(1,128)} %bitcast.8, f32[4096,128]{1,0:T(8,128)} %load_ref.3, f32[4096,128]{1,0:T(8,128)} %get-tuple-element.16.y_ref, f32[128,128]{1,0:T(8,128)} %get-tuple-element.17.z_ref), custom_call_target="tpu_custom_call" | custom-call | tf_op jit(solution)/shard_map/second_pass/pallas_call | solution.py:118
  74.2 0.0 copy-start
  74.2 48.1 %core_sums.1.sums_ref = f32[768,128]{1,0:T(8,128)} custom-call(f32[128,2048]{1,0:T(8,128)} %get-tuple-element.18.d_in, f32[128,256]{1,0:T(8,128)} %get-tuple-element.19.p_ref, f32[256,128]{1,0:T(8,128)} %get-tuple-element.20.ga_ref), custom_call_target="tpu_custom_call" | custom-call | tf_op jit(solution)/shard_map/core_sums/pallas_call | solution.py:367
  122.2 50.0 %small.1 = (f32[256,128]{1,0:T(8,128)}, f32[1,128]{1,0:T(1,128)}) custom-call(f32[768,128]{1,0:T(8,128)} %core_sums.1.sums_ref, f32[1,128]{1,0:T(1,128)} %bitcast.9), custom_call_target="tpu_custom_call" | custom-call | tf_op jit(solution)/shard_map/small/pallas_call | solution.py:456
  172.2 0.0 copy-done
  172.2 0.0 copy-start.1
  172.2 0.0 copy-start.2
  172.2 2.9 %convolution_bitcast_fusion = f32[4096,128]{0,1:T(8,128)S(1)} fusion(f32[4096,128]{1,0:T(8,128)S(1)} %copy-done, f32[256,128]{1,0:T(8,128)} %get-tuple-element.21), kind=kOutput, calls=%fused_computation.2 | convolution fusion | flops 805306368 | bytes 4259840 | tf_op jit(solution)/shard_map/dot_general | solution.py:485
  175.2 0.0 copy-done.1
  175.2 0.0 copy-done.2
  175.2 2.2 %fusion = f32[4096,128]{0,1:T(8,128)S(1)} fusion(f32[4096,128]{0,1:T(8,128)S(1)} %convolution_bitcast_fusion, f32[4096,128]{1,0:T(8,128)S(1)} %copy-done.1, f32[256,128]{1,0:T(8,128)S(1)} %copy-done.2), kind=kOutput, calls=%fused_computation.1 | convolution fusion | flops 806354944 | bytes 6356992 | tf_op jit(solution)/shard_map/dot_general | solution.py:485
  177.4 1.8 %copy.8 = f32[4096,128]{1,0:T(8,128)} copy(f32[4096,128]{0,1:T(8,128)S(1)} %fusion) | data formatting | bytes 4194304
Async XLA Ops:
  74.2 98.1 %copy-start = (f32[4096,128]{1,0:T(8,128)S(1)}, f32[4096,128]{1,0:T(8,128)}, u32[]{:S(2)}) copy-start(f32[4096,128]{1,0:T(8,128)} %load_ref.3) | copy-start | bytes 6291460
  172.2 3.0 %copy-start.1 = (f32[4096,128]{1,0:T(8,128)S(1)}, f32[4096,128]{1,0:T(8,128)}, u32[]{:S(2)}) copy-start(f32[4096,128]{1,0:T(8,128)} %get-tuple-element.22) | copy-start | bytes 6291460
  172.2 3.0 %copy-start.2 = (f32[256,128]{1,0:T(8,128)S(1)}, f32[256,128]{1,0:T(8,128)}, u32[]{:S(2)}) copy-start(f32[256,128]{1,0:T(8,128)} %get-tuple-element.21) | copy-start | bytes 393220

commit v2 on v1

--- a/solution.py
+++ b/solution.py
@@ -13,6 +13,7 @@
 ROW_BLOCK = 512
 CHUNKS = 8
 HIGH = lax.Precision.HIGHEST
+GROUP = 8
 MESH = pl.DeviceIdType.MESH
 LIMIT = 60 * 1024 * 1024
 VMEM = pl.BlockSpec(memory_space=pltpu.VMEM)
@@ -27,6 +28,14 @@
 def split(a):
     high = a.astype(jnp.bfloat16)
     return high, (a - high.astype(jnp.float32)).astype(jnp.bfloat16)
+
+
+def dot_split(a, b):
+    return (
+        dot(a[0], b[0], precision=None)
+        + dot(a[0], b[1], precision=None)
+        + dot(a[1], b[0], precision=None)
+    )
 
 
 def masked_rows(counts_ref, mask_ref, step):
@@ -87,36 +96,39 @@
     )(counts, mask_rows, loadings, test_matrix)
 
 
-def second_kernel(share, counts_ref, mask_ref, load_ref, y_ref, z_ref, s_ref, d_ref, ga_ref):
+def second_kernel(steps, counts_ref, mask_ref, load_ref, y_ref, z_ref, s_ref, d_ref, ga_ref):
     step = pl.program_id(0)
     masked = masked_rows(counts_ref, mask_ref, step)
     load = load_ref[...]
-    sketch = y_ref[...] - dot(load, z_ref[...])
+    sketch = y_ref[...] - dot_split(split(load), split(z_ref[...]))
     s_ref[...] = sketch
     high, low = split(sketch)
     both = dot(jnp.concatenate([high, low], axis=1), masked, ((0,), (0,)), None)
     width = sketch.shape[1]
     part = both[:width] + both[width:]
-    small = (
-        dot(jnp.concatenate([sketch, load], axis=1), sketch, ((0,), (0,))) * share
-    )
 
     @pl.when(step == 0)
     def _():
         d_ref[...] = part
-        ga_ref[...] = small
+        ga_ref[...] = jnp.zeros_like(ga_ref)
 
     @pl.when(step > 0)
     def _():
         d_ref[...] += part
-        ga_ref[...] += small
-
-
-def second_pass(counts, mask_rows, loadings, y, z, share):
+
+    cells = lax.axis_size("cell")
+    every = pl.cdiv(steps, cells)
+
+    @pl.when(step // every == lax.axis_index("cell"))
+    def _():
+        ga_ref[...] += dot(jnp.concatenate([sketch, load], axis=1), sketch, ((0,), (0,)))
+
+
+def second_pass(counts, mask_rows, loadings, y, z):
     rows, cols = counts.shape
     comps, width = loadings.shape[1], y.shape[1]
     return pl.pallas_call(
-        functools.partial(second_kernel, share),
+        functools.partial(second_kernel, rows // ROW_BLOCK),
         grid=(rows // ROW_BLOCK,),
         in_specs=[
             pl.BlockSpec((ROW_BLOCK, cols), lambda i: (i, 0)),
@@ -198,10 +210,109 @@
     return ref.at[:, pl.ds(pl.multiple_of(index * count, 128), count)]
 
 
+class Scatter:
+    def __init__(self, gene, source, pair_slots, slots, pair_sems, sems):
+        self.gene, self.source = gene, source
+        self.pair_slots, self.slots = pair_slots, slots
+        self.pair_sems, self.sems = pair_sems, sems
+        self.wide = source.shape[1] // gene.size
+        self.half = gene.size // 2
+        self.parity = lax.rem(gene.me, 2)
+        self.place = gene.me // 2
+        self.owners = [lax.rem(self.place + 1 + o, self.half) for o in range(self.half)]
+
+    def copy(self, source, target, sems, index, device):
+        copy = pltpu.make_async_remote_copy(
+            src_ref=source,
+            dst_ref=target,
+            send_sem=sems.at[0, index],
+            recv_sem=sems.at[1, index],
+            device_id={"gene": device},
+            device_id_type=MESH,
+        )
+        copy.start()
+        return copy
+
+    def start(self):
+        partner = self.gene.me + 1 - 2 * self.parity
+        self.pairs = [
+            self.copy(
+                cols_of(self.source, 2 * q + 1 - self.parity, self.wide),
+                self.pair_slots.at[q], self.pair_sems, o, partner,
+            )
+            for o, q in enumerate(self.owners)
+        ]
+
+    def relay(self):
+        self.across = []
+        for o, q in enumerate(self.owners):
+            self.pairs[o].wait_recv()
+            own = 2 * q + self.parity
+            total = cols_of(self.source, own, self.wide)[...] + self.pair_slots[q]
+            if o == self.half - 1:
+                self.slots[q] = total
+            else:
+                self.pair_slots[q] = total
+                self.across.append(
+                    self.copy(
+                        self.pair_slots.at[q], self.slots.at[self.place], self.sems, o, own
+                    )
+                )
+
+    def finish(self):
+        received(self.across)
+        return ordered_sum(self.slots, self.half)
+
+    def sent(self):
+        sent(self.pairs + self.across)
+
+
+class AllSum:
+    def __init__(self, gene, cell, parts, out, c_slots, g_slots, sems):
+        self.gene, self.cell, self.parts, self.out = gene, cell, parts, out
+        self.c_slots, self.g_slots, self.sems = c_slots, g_slots, sems
+        self.c_rows = parts.shape[0] // cell.size
+        self.g_rows = self.c_rows // gene.size
+
+    def start(self):
+        cell = self.cell
+        self.first = cell.send(
+            lambda q: rows_of(self.parts, q, self.c_rows), self.c_slots.at[cell.me], self.sems[0]
+        )
+        self.c_slots[cell.me] = rows_of(self.parts, cell.me, self.c_rows)[...]
+
+    def over_gene(self):
+        gene, cell = self.gene, self.cell
+        received(self.first)
+        sent(self.first)
+        mine = rows_of(self.parts, cell.me, self.c_rows)
+        mine[...] = ordered_sum(self.c_slots, cell.size)
+        self.second = gene.send(
+            lambda q: rows_of(mine, q, self.g_rows), self.g_slots.at[gene.me], self.sems[1]
+        )
+        self.g_slots[gene.me] = rows_of(mine, gene.me, self.g_rows)[...]
+
+    def back_gene(self):
+        gene, cell = self.gene, self.cell
+        received(self.second)
+        done = rows_of(rows_of(self.out, cell.me, self.c_rows), gene.me, self.g_rows)
+        done[...] = ordered_sum(self.g_slots, gene.size)
+        self.third = gene.send(lambda q: done, done, self.sems[2])
+
+    def back_cell(self):
+        received(self.third)
+        block = rows_of(self.out, self.cell.me, self.c_rows)
+        self.fourth = self.cell.send(lambda q: block, block, self.sems[3])
+
+    def finish(self):
+        received(self.fourth)
+        sent(self.second + self.third + self.fourth)
+
+
 def gather_kernel(
     y_in, p_in, z_in, y_out, p_out, z_out,
-    z_cell, z_gene, p_slots, pair_slots, chip_slots,
-    zc_sems, zg_sems, za_sems, p_sems, pair_sems, chip_sems, back_sems,
+    z_cell, z_gene, p_pairs, p_slots, pair_slots, chip_slots,
+    zc_sems, zg_sems, za_sems, pp_sems, p_sems, pair_sems, chip_sems, back_sems,
 ):
     gene, cell = Group("gene"), Group("cell")
     barrier = pltpu.get_barrier_semaphore()
@@ -214,7 +325,7 @@
     half = rows // 2
     chunk = half // CHUNKS
     zrows = z_in.shape[0] // cell.size
-    wide = p_in.shape[1] // gene.size
+    scatter = Scatter(gene, p_in, p_pairs, p_slots, pp_sems, p_sems)
 
     def to(device, source, target, sems, *index):
         copy = pltpu.make_async_remote_copy(
@@ -228,7 +339,6 @@
         copy.start()
         return copy
 
-    pending = []
     z_first = cell.send(lambda q: rows_of(z_in, q, zrows), z_cell.at[cell.me], zc_sems)
     z_cell[cell.me] = rows_of(z_in, cell.me, zrows)[...]
     pairs = []
@@ -241,8 +351,7 @@
     received(z_first)
     z_gene[gene.me] = ordered_sum(z_cell, cell.size)
     z_second = gene.send(lambda q: z_gene.at[gene.me], z_gene.at[gene.me], zg_sems)
-    p_copies = gene.send(lambda q: cols_of(p_in, q, wide), p_slots.at[gene.me], p_sems)
-    p_slots[gene.me] = cols_of(p_in, gene.me, wide)[...]
+    scatter.start()
     across = []
     for j in range(CHUNKS):
         start = pl.multiple_of(core * half + j * chunk, 8)
@@ -253,6 +362,7 @@
         for offset in range(1, chips):
             other = lax.rem(chip + offset, chips) * 2 + core
             across.append(to(other, block, block, chip_sems, offset, j))
+    scatter.relay()
     received(z_second)
     rows_of(z_out, cell.me, zrows)[...] = ordered_sum(z_gene, gene.size)
     block = rows_of(z_out, cell.me, zrows)
@@ -269,10 +379,10 @@
         block = y_out.at[pl.ds(start, chunk), :]
         backs.append(to(partner, block, block, back_sems, j))
     received(z_third)
-    received(p_copies)
-    p_out[...] = ordered_sum(p_slots, gene.size)
+    p_out[...] = scatter.finish()
     received(backs)
-    sent(z_first + pairs + z_second + p_copies + across + z_third + backs)
+    scatter.sent()
+    sent(z_first + pairs + z_second + across + z_third + backs)
 
 
 def gather(y, p, z):
@@ -292,13 +402,15 @@
         scratch_shapes=[
             pltpu.VMEM((cells, comps // cells, width), jnp.float32),
             pltpu.VMEM((genes, comps // cells, width), jnp.float32),
-            pltpu.VMEM((genes, comps, cols // genes), jnp.float32),
+            pltpu.VMEM((genes // 2, comps, cols // genes), jnp.float32),
+            pltpu.VMEM((genes // 2, comps, cols // genes), jnp.float32),
             pltpu.VMEM((rows // 2, width), jnp.float32),
             pltpu.VMEM((cells // 2, rows // 2, width), jnp.float32),
             dma((2, cells)),
             dma((2, genes)),
             dma((2, cells)),
-            dma((2, genes)),
+            dma((2, genes // 2)),
+            dma((2, genes // 2)),
             dma((2, CHUNKS)),
             dma((2, cells // 2, CHUNKS)),
             dma((2, CHUNKS)),
@@ -311,50 +423,41 @@
 
 
 def core_kernel(
-    d_in, p_ref, ga_ref, out_ref,
-    d_slots, parts, c_slots, g_slots,
-    d_sems, c_sems, g_sems, ga_sems, ca_sems,
+    d_in, p_ref, ga_ref, early_out, late_out,
+    d_pairs, d_slots, early, late, ec_slots, eg_slots, lc_slots, lg_slots,
+    pair_sems, d_sems, *sems,
 ):
     gene, cell = Group("gene"), Group("cell")
     barrier = pltpu.get_barrier_semaphore()
     pl.semaphore_wait(barrier, gene.greet(barrier) + cell.greet(barrier))
-    wide = d_in.shape[1] // gene.size
-    d_copies = gene.send(lambda q: cols_of(d_in, q, wide), d_slots.at[gene.me], d_sems)
-    d_slots[gene.me] = cols_of(d_in, gene.me, wide)[...]
+    scatter = Scatter(gene, d_in, d_pairs, d_slots, pair_sems, d_sems)
+    scatter.start()
     proj = p_ref[...]
     comps = proj.shape[0]
-    width = d_in.shape[0]
-    total_rows = parts.shape[0]
-    small = 3 * comps + ga_ref.shape[0]
-    parts[pl.ds(0, comps), :] = dot(proj, proj, ((1,), (1,)))
-    parts[pl.ds(3 * comps, ga_ref.shape[0]), :] = ga_ref[...]
-    if total_rows > small:
-        parts[pl.ds(small, total_rows - small), :] = jnp.zeros(
-            (total_rows - small, comps), jnp.float32
-        )
-    received(d_copies)
-    inner = ordered_sum(d_slots, gene.size)
-    parts[pl.ds(comps, comps), :] = dot(proj, inner, ((1,), (1,)))
-    parts[pl.ds(2 * comps, width), :] = dot(inner, inner, ((1,), (1,)))
-    c_rows = total_rows // cell.size
-    g_rows = c_rows // gene.size
-    first = cell.send(lambda q: rows_of(parts, q, c_rows), c_slots.at[cell.me], c_sems)
-    c_slots[cell.me] = rows_of(parts, cell.me, c_rows)[...]
-    received(first)
-    sent(first)
-    mine = rows_of(parts, cell.me, c_rows)
-    mine[...] = ordered_sum(c_slots, cell.size)
-    second = gene.send(lambda q: rows_of(mine, q, g_rows), g_slots.at[gene.me], g_sems)
-    g_slots[gene.me] = rows_of(mine, gene.me, g_rows)[...]
-    received(second)
-    done = rows_of(rows_of(out_ref, cell.me, c_rows), gene.me, g_rows)
-    done[...] = ordered_sum(g_slots, gene.size)
-    third = gene.send(lambda q: done, done, ga_sems)
-    received(third)
-    block = rows_of(out_ref, cell.me, c_rows)
-    fourth = cell.send(lambda q: block, block, ca_sems)
-    received(fourth)
-    sent(d_copies + second + third + fourth)
+    small = ga_ref.shape[0]
+    early[pl.ds(0, comps), :] = dot(proj, proj, ((1,), (1,)))
+    early[pl.ds(comps, small), :] = ga_ref[...]
+    for ref, used in ((early, comps + small), (late, 2 * comps)):
+        rest = ref.shape[0] - used
+        if rest:
+            ref[pl.ds(used, rest), :] = jnp.zeros((rest, comps), jnp.float32)
+    first = AllSum(gene, cell, early, early_out, ec_slots, eg_slots, sems[:4])
+    second = AllSum(gene, cell, late, late_out, lc_slots, lg_slots, sems[4:])
+    first.start()
+    scatter.relay()
+    first.over_gene()
+    inner = scatter.finish()
+    late[pl.ds(0, comps), :] = dot(proj, inner, ((1,), (1,)))
+    late[pl.ds(comps, comps), :] = dot(inner, inner, ((1,), (1,)))
+    second.start()
+    first.back_gene()
+    second.over_gene()
+    first.back_cell()
+    second.back_gene()
+    second.back_cell()
+    first.finish()
+    second.finish()
+    scatter.sent()
 
 
 def core_sums(d, p, ga):
@@ -362,23 +465,36 @@
     comps, wide = p.shape
     width = d.shape[0]
     unit = 8 * genes * cells
-    total_rows = -(-(3 * comps + ga.shape[0]) // unit) * unit
+    early = -(-(comps + ga.shape[0]) // unit) * unit
+    late = -(-(2 * comps) // unit) * unit
     dma = pltpu.SemaphoreType.DMA
+
+    def slots(rows):
+        return [
+            pltpu.VMEM((cells, rows // cells, comps), jnp.float32),
+            pltpu.VMEM((genes, rows // cells // genes, comps), jnp.float32),
+        ]
+
+    sems = [dma((2, cells)), dma((2, genes)), dma((2, genes)), dma((2, cells))]
     return pl.pallas_call(
         core_kernel,
         in_specs=[VMEM] * 3,
-        out_specs=VMEM,
-        out_shape=jax.ShapeDtypeStruct((total_rows, comps), jnp.float32),
+        out_specs=[VMEM] * 2,
+        out_shape=[
+            jax.ShapeDtypeStruct((early, comps), jnp.float32),
+            jax.ShapeDtypeStruct((late, comps), jnp.float32),
+        ],
         scratch_shapes=[
-            pltpu.VMEM((genes, width, wide), jnp.float32),
-            pltpu.VMEM((total_rows, comps), jnp.float32),
-            pltpu.VMEM((cells, total_rows // cells, comps), jnp.float32),
-            pltpu.VMEM((genes, total_rows // cells // genes, comps), jnp.float32),
-            dma((2, genes)),
-            dma((2, cells)),
-            dma((2, genes)),
-            dma((2, genes)),
-            dma((2, cells)),
+            pltpu.VMEM((genes // 2, width, wide), jnp.float32),
+            pltpu.VMEM((genes // 2, width, wide), jnp.float32),
+            pltpu.VMEM((early, comps), jnp.float32),
+            pltpu.VMEM((late, comps), jnp.float32),
+            *slots(early),
+            *slots(late),
+            dma((2, genes // 2)),
+            dma((2, genes // 2)),
+            *sems,
+            *sems,
         ],
         compiler_params=pltpu.CompilerParams(
             collective_id=2, has_side_effects=True, vmem_limit_bytes=LIMIT
@@ -389,19 +505,50 @@
 
 def inverse_factor(gram):
     order = gram.shape[0]
-    lane = lax.broadcasted_iota(jnp.int32, (1, order), 1)
-    below = lax.broadcasted_iota(jnp.int32, (8, 1), 0)
-    blocks = [gram[8 * b:8 * b + 8] for b in range(order // 8)]
-    for k in range(order):
+    shape = (8, order)
+    lane = lax.broadcasted_iota(jnp.int32, shape, 1)
+    sub = lax.broadcasted_iota(jnp.int32, shape, 0)
+    count = order // 8
+    blocks = [gram[8 * b:8 * b + 8] for b in range(count)]
+    for k in range(0, order, GROUP):
         home, spot = k // 8, k % 8
-        pivot_row = blocks[home][spot:spot + 1]
-        scaled = jnp.where(lane == k, 1.0, pivot_row) * (1.0 / pivot_row[:, k:k + 1])
-        for b in range(home, order // 8):
-            column = blocks[b][:, k:k + 1]
-            kept = jnp.where(lane == k, 0.0, blocks[b])
-            changed = kept - column * scaled
+        last = k + GROUP - 1
+        columns = {
+            b: [jnp.broadcast_to(blocks[b][:, k + i:k + i + 1], shape) for i in range(GROUP)]
+            for b in range(home, count)
+        }
+        rows = [
+            jnp.broadcast_to(blocks[home][spot + i:spot + i + 1], shape) for i in range(GROUP)
+        ]
+        entry = [
+            [jnp.broadcast_to(rows[i][:, k + j:k + j + 1], shape) for j in range(GROUP)]
+            for i in range(GROUP)
+        ]
+        scaled = []
+        for i in range(GROUP):
+            inverse = 1.0 / entry[i][i]
+            row = jnp.where(lane == k + i, 1.0, rows[i]) * inverse
+            ratio = [entry[i][m] * inverse for m in range(GROUP)]
+            for j in range(i + 1, GROUP):
+                rows[j] = jnp.where(lane == k + i, 0.0, rows[j]) - entry[j][i] * row
+                for m in range(i + 1, GROUP):
+                    entry[j][m] = entry[j][m] - entry[j][i] * ratio[m]
+            for b in range(home, count):
+                for m in range(i + 1, GROUP):
+                    columns[b][m] = columns[b][m] - columns[b][i] * ratio[m]
+            scaled.append(jnp.where((lane > k + i) & (lane <= last), 0.0, row))
+        inside = (lane >= k) & (lane <= last)
+        for b in range(home, count):
+            if b == home and spot + GROUP == 8:
+                changed = blocks[b]
+            else:
+                changed = jnp.where(inside, 0.0, blocks[b])
+                for i in range(GROUP):
+                    changed = changed - columns[b][i] * scaled[i]
             if b == home:
-                changed = jnp.where(below > spot, changed, blocks[b])
+                changed = jnp.where(sub < spot, blocks[b], changed)
+                for i in range(GROUP):
+                    changed = jnp.where(sub == spot + i, rows[i], changed)
             blocks[b] = changed
     full = jnp.concatenate(blocks, axis=0)
     row = lax.broadcasted_iota(jnp.int32, (order, order), 0)
@@ -411,13 +558,16 @@
     return unit * lax.rsqrt(pivots)
 
 
-def small_kernel(cells_total, sums_ref, values_ref, mix_ref, new_values_ref, core_ref, sub_ref, inv_ref):
+def small_kernel(
+    cells_total, root, early_ref, late_ref, values_ref,
+    mix_ref, new_values_ref, core_ref, sub_ref, inv_ref,
+):
     comps = values_ref.shape[1]
-    pp = sums_ref[pl.ds(0, comps), :]
-    pd = sums_ref[pl.ds(comps, comps), :]
-    dd = sums_ref[pl.ds(2 * comps, comps), :]
-    gram = sums_ref[pl.ds(3 * comps, comps), :]
-    along_t = sums_ref[pl.ds(4 * comps, comps), :]
+    pp = early_ref[pl.ds(0, comps), :]
+    gram = early_ref[pl.ds(comps, comps), :]
+    along_t = early_ref[pl.ds(2 * comps, comps), :]
+    pd = late_ref[pl.ds(0, comps), :]
+    dd = late_ref[pl.ds(comps, comps), :]
     inv_ref[...] = inverse_factor(gram)
     inv = inv_ref[...]
     cross = dot(pd, along_t, ((0,), (0,)))
@@ -447,15 +597,15 @@
     sub = sub_ref[...]
     image = dot(core_ref[...], sub)
     new_values_ref[...] = jnp.sqrt(jnp.sum(sub * image, axis=0, keepdims=True))
-    mix_ref[pl.ds(0, comps), :] = sub[:comps]
-    mix_ref[pl.ds(comps, comps), :] = dot(inv_ref[...], sub[comps:], ((0,), (0,)))
-
-
-def small(sums, values, cells_total):
+    mix_ref[pl.ds(0, comps), :] = sub[:comps] * root
+    mix_ref[pl.ds(comps, comps), :] = dot(inv_ref[...], sub[comps:], ((0,), (0,))) * root
+
+
+def small(early, late, values, cells_total, root):
     comps = values.shape[0]
     return pl.pallas_call(
-        functools.partial(small_kernel, cells_total),
-        in_specs=[VMEM] * 2,
+        functools.partial(small_kernel, cells_total, root),
+        in_specs=[VMEM] * 3,
         out_specs=[VMEM] * 2,
         out_shape=[
             jax.ShapeDtypeStruct((2 * comps, comps), jnp.float32),
@@ -467,7 +617,25 @@
             pltpu.VMEM((comps, comps), jnp.float32),
         ],
         name="small",
-    )(sums, values.reshape(1, comps))
+    )(early, late, values.reshape(1, comps))
+
+
+def last_kernel(load_ref, sketch_ref, mix_ref, out_ref):
+    both = jnp.concatenate([load_ref[...], sketch_ref[...]], axis=1)
+    out_ref[...] = dot_split(split(both), split(mix_ref[...]))
+
+
+def last_pass(loadings, sketch, mix):
+    rows, comps = loadings.shape
+    block = pl.BlockSpec((2 * ROW_BLOCK, comps), lambda i: (i, 0))
+    return pl.pallas_call(
+        last_kernel,
+        grid=(rows // (2 * ROW_BLOCK),),
+        in_specs=[block, block, pl.BlockSpec(mix.shape, lambda i: (0, 0))],
+        out_specs=block,
+        out_shape=jax.ShapeDtypeStruct((rows, comps), jnp.float32),
+        name="last_pass",
+    )(loadings, sketch, mix)
 
 
 def local(counts, loadings, values, test_matrix, tile_mask):
@@ -478,14 +646,10 @@
     mask_rows = jnp.repeat(tile_mask.astype(jnp.float32), CELL_TILE, axis=1)[:, None, :]
     y, p, z = first_pass(counts, mask_rows, loadings, test_matrix)
     y, p, z = gather(y, p, z)
-    sketch, d, ga = second_pass(counts, mask_rows, loadings, y, z, 1.0 / cells)
-    sums = core_sums(d, p, ga)
-    mix, new_values = small(sums, values, cell_cols * cells)
-    root = genes_total**0.5
-    rotated = jnp.dot(loadings, mix[:comps], precision=HIGH) + jnp.dot(
-        sketch, mix[comps:], precision=HIGH
-    )
-    return rotated * root, new_values.reshape(comps)
+    sketch, d, ga = second_pass(counts, mask_rows, loadings, y, z)
+    early, late = core_sums(d, p, ga)
+    mix, new_values = small(early, late, values, cell_cols * cells, genes_total**0.5)
+    return last_pass(loadings, sketch, mix), new_values.reshape(comps)
 
 
 def solution(mesh):

time: 180 us -> 142 us (0.79)
  Pallas kernels: 170 us -> 139 us
  matrix products: 5.09 us -> 0 us
  local copies, waits for them, and re-layouts: 2.57 us -> 0.75 us
    pallas_call x3 -> x4, Pallas kernels: 117 us -> 85.8 us  [the longest x1 38.3 us: core_sums(): pl.pallas_call(core_kernel, in_specs=[VMEM] * 3, out_specs=[VMEM] * 2, ou...]
    dot_general x2 -> x0, matrix products: 5.09 us -> none  [the longest x1 2.94 us: local(): jnp.dot(loadings, mix[:comps], precision=HIGH)]
    unnamed x7 -> x0, local copies, waits for them, and re-layouts: 1.82 us -> none
where the time goes in v2:
time: 142 us; the launch traced here: 141 us
  Pallas kernels  139 us (98%)
    pallas_call x1, Pallas kernels, gather(): pl.pallas_call(gather_kernel, in_specs=[VMEM] * 3, out_specs=[VMEM] * 3,...  38.9 us
    pallas_call x1, Pallas kernels, core_sums(): pl.pallas_call(core_kernel, in_specs=[VMEM] * 3, out_specs=[VMEM] * 2, ou...  38.3 us
    pallas_call x1, Pallas kernels, small(): pl.pallas_call(functools.partial(small_kernel, cells_total, root), in_spe...  26.5 us
    pallas_call x1, Pallas kernels, second_pass(): pl.pallas_call(functools.partial(second_kernel, rows // ROW_BLOCK), grid=...  15.8 us
    pallas_call x1, Pallas kernels, first_pass(): pl.pallas_call(first_kernel, grid=(rows // ROW_BLOCK,), in_specs=[pl.Bloc...  14.2 us
    pallas_call x1, Pallas kernels, last_pass(): pl.pallas_call(last_kernel, grid=(rows // (2 * ROW_BLOCK),), in_specs=[bl...  5.26 us

profile of v2, /device:TPU:0, one launch (start us, length us, event | category | flops | bytes accessed | tf_op | source)
XLA Modules:
  0.0 141.0 jit_solution(10308264569147864582)
XLA Ops:
  0.6 0.7 convert_element_type.3
  1.3 0.7 broadcast_in_dim.3
  2.1 14.2 %first_pass.1 = (f32[4096,128]{1,0:T(8,128)}, f32[128,2048]{1,0:T(8,128)}, f32[128,128]{1,0:T(8,128)}) custom-call(bf16[4096,2048]{1,0:T(8,128)(2,1)} %counts_ref.3, f32[16,1,2048]{2,1,0:T(1,128)} %bitcast.3, f32[4096,128]{1,0:T(8,128)} %load_ref.5, bf16[2048,128]{1,0:T(8,128)(2,1)} %test_ref.1), custom_call_target="tpu_custom_call" | custom-call | tf_op jit(solution)/shard_map/first_pass/pallas_call | solution.py:75
  16.3 38.9 %gather.1 = (f32[4096,128]{1,0:T(8,128)}, f32[128,256]{1,0:T(8,128)}, f32[128,128]{1,0:T(8,128)}) custom-call(f32[4096,128]{1,0:T(8,128)} %get-tuple-element.15.y_in, f32[128,2048]{1,0:T(8,128)} %get-tuple-element.16.p_in, f32[128,128]{1,0:T(8,128)} %get-tuple-element.17.z_in), custom_call_target="tpu_custom_call" | custom-call | tf_op jit(solution)/shard_map/gather/pallas_call | solution.py:393
  55.2 15.8 %second_pass.1 = (f32[4096,128]{1,0:T(8,128)}, f32[128,2048]{1,0:T(8,128)}, f32[256,128]{1,0:T(8,128)}) custom-call(bf16[4096,2048]{1,0:T(8,128)(2,1)} %counts_ref.3, f32[16,1,2048]{2,1,0:T(1,128)} %bitcast.4, f32[4096,128]{1,0:T(8,128)} %load_ref.5, f32[4096,128]{1,0:T(8,128)} %get-tuple-element.18.y_ref, f32[128,128]{1,0:T(8,128)} %get-tuple-element.19.z_ref), custom_call_target="tpu_custom_call" | custom-call | tf_op jit(solution)/shard_map/second_pass/pallas_call | solution.py:130
  71.0 38.3 %core_sums.1 = (f32[512,128]{1,0:T(8,128)}, f32[256,128]{1,0:T(8,128)}) custom-call(f32[128,2048]{1,0:T(8,128)} %get-tuple-element.21.d_in, f32[128,256]{1,0:T(8,128)} %get-tuple-element.22.p_ref, f32[256,128]{1,0:T(8,128)} %get-tuple-element.23.ga_ref), custom_call_target="tpu_custom_call" | custom-call | tf_op jit(solution)/shard_map/core_sums/pallas_call | solution.py:479
  109.2 26.5 %small.1 = (f32[256,128]{1,0:T(8,128)}, f32[1,128]{1,0:T(1,128)}) custom-call(f32[512,128]{1,0:T(8,128)} %get-tuple-element.24.early_ref, f32[256,128]{1,0:T(8,128)} %get-tuple-element.25.late_ref, f32[1,128]{1,0:T(1,128)} %bitcast.5), custom_call_target="tpu_custom_call" | custom-call | tf_op jit(solution)/shard_map/small/pallas_call | solution.py:606
  135.8 5.3 %last_pass.1 = f32[4096,128]{1,0:T(8,128)} custom-call(f32[4096,128]{1,0:T(8,128)} %load_ref.5, f32[4096,128]{1,0:T(8,128)} %get-tuple-element.20.sketch_ref, f32[256,128]{1,0:T(8,128)} %get-tuple-element.26.mix_ref), custom_call_target="tpu_custom_call" | custom-call | tf_op jit(solution)/shard_map/last_pass/pallas_call | solution.py:631
